TPU v7x, 32 devices: a whole 2x2x4 slice. The times are simulated.
32 devices in a mesh: groups: 2 (over x), sph: 16 (over z, y, core).
Axes of the slice: x: 2, y: 2, z: 4, core: 2. Of those that a mesh axis runs over, the one named last changes fastest.
Arguments:
- positions: float32 [512, 3], P('sph'), may hold values from -8 to 8
- wave_vectors: float32 [256, 3], replicated, may hold values from -5 to 5
- pattern: float32 [2, 448, 256], replicated, may hold values from -6 to 6
- dir_index: int32 [64], P('groups'), parts along dimension 0, may hold values from 0 to 255
- mie: float32 [2, 448, 512], P(None, None, 'sph'), may hold values from -0.9 to 0.9
- trans_table: bfloat16 [8, 2, 448, 448], replicated, may hold values from -0.1875 to 0.1875
- pair_route: int32 [1024, 1], P('sph'), may hold values from 0 to 15; in each aligned block of 64 rows (0 to 63, 64 to 127, ...) at most 8 rows name the same one
- pair_source: int32 [1024], P('sph'), may hold values from 0 to 15
- pair_target: int32 [1024], P('sph'), may hold values from 0 to 15
- pair_class: int32 [1024], P('sph'), may hold values from 0 to 7
Outputs:
- scattered: bfloat16 [896, 32768], P(None, ('groups', 'sph')), parts along dimension 1
- extinction: float32 [64], P('groups'), parts along dimension 0
There are 2 independent parts, one for each index of `groups`. A program takes and returns all parts, laid end to end along the dimension named above; an argument that names none is the same for every part. Nothing has to cross between parts.
Inputs may be any that keep to these rules, and one draw needn't show every extreme that they name: `pair_route`: among the rows of one device no device is named by more than 8 pairs, and in every draw some device is named by exactly 8 of them.
All inputs are finite; a program needn't handle non-finite values.
Results may differ from a plain program's by a relative error of at most 0.0051.
Values may be sent and summed in bfloat16 or wider, within the bound.
No kernel may reach another device: no remote copies, remote signals or barrier semaphores. Data moves between devices by JAX's collectives and lax.ppermute only.
A program may use at most 192 MiB of HBM per device.

v0:
```python
import jax
import jax.numpy as jnp
from jax import lax
from jax.sharding import PartitionSpec as P

BLOCK = 2
HIGHEST_PRECISION = lax.Precision.HIGHEST


def incident_field(positions, wave_vectors, pattern, dir_index):
    table_rows = wave_vectors.shape[0]
    select = (jnp.arange(table_rows, dtype=jnp.int32)[:, None] == dir_index[None, :]).astype(
        jnp.float32
    )
    directions = jnp.dot(select.T, wave_vectors, precision=HIGHEST_PRECISION)
    phases = (
        positions[:, 0:1] * directions[None, :, 0]
        + positions[:, 1:2] * directions[None, :, 1]
        + positions[:, 2:3] * directions[None, :, 2]
    )
    cosine = jnp.cos(phases)
    sine_part = jnp.sin(phases)
    chosen = jnp.einsum("cmt,td->cmd", pattern, select, precision=HIGHEST_PRECISION)
    inc_real = cosine[None] * chosen[0][:, None, :] - sine_part[None] * chosen[1][:, None, :]
    inc_imag = cosine[None] * chosen[1][:, None, :] + sine_part[None] * chosen[0][:, None, :]
    return (inc_real, inc_imag)


def translate(trans_table, classes, block_values):
    item_count = classes.shape[0]
    mode_count = trans_table.shape[2]
    grouped_classes = classes.reshape(item_count // 8, 8)
    grouped_values = block_values.reshape((item_count // 8, 8) + block_values.shape[1:])

    def one_group(group_items):
        picked, values = group_items
        tables = trans_table[picked]
        data_real = values[:, :mode_count]
        data_imag = values[:, mode_count:]
        part_real = jnp.einsum(
            "kij,kjc->kic", tables[:, 0], data_real, preferred_element_type=jnp.float32
        ) - jnp.einsum("kij,kjc->kic", tables[:, 1], data_imag, preferred_element_type=jnp.float32)
        part_imag = jnp.einsum(
            "kij,kjc->kic", tables[:, 1], data_real, preferred_element_type=jnp.float32
        ) + jnp.einsum("kij,kjc->kic", tables[:, 0], data_imag, preferred_element_type=jnp.float32)
        return jnp.concatenate([part_real, part_imag], 1).astype(jnp.bfloat16)

    return lax.map(one_group, (grouped_classes, grouped_values)).reshape(block_values.shape)


def shards(
    positions,
    wave_vectors,
    pattern,
    dir_index,
    mie,
    trans_table,
    pair_route,
    pair_source,
    pair_target,
    pair_class,
):
    mode_count = pattern.shape[1]
    spheres = positions.shape[0]
    directions = dir_index.shape[0]
    columns = BLOCK * directions
    block_count = spheres // BLOCK
    devices = lax.axis_size("sph")
    pair_count = pair_source.shape[0]
    capacity = max(2, 2 * pair_count // devices)
    slot_count = devices * capacity
    inc_real, inc_imag = incident_field(positions, wave_vectors, pattern, dir_index)
    mie_real = mie[0][:, :, None]
    mie_imag = mie[1][:, :, None]
    scat_real = mie_real * inc_real - mie_imag * inc_imag
    scat_imag = mie_real * inc_imag + mie_imag * inc_real
    coeffs = jnp.concatenate([scat_real, scat_imag], 0).astype(jnp.bfloat16)
    block_data = coeffs.reshape(2 * mode_count, block_count, columns).transpose(1, 0, 2)
    dest_device = pair_route[:, 0]
    by_device = (dest_device[:, None] == jnp.arange(devices, dtype=jnp.int32)[None, :]).astype(
        jnp.int32
    )
    before = jnp.cumsum(by_device, axis=0) - by_device
    rank_in = jnp.sum(before * by_device, axis=1)
    slot_of = dest_device * capacity + rank_in
    slot_match = (jnp.arange(slot_count, dtype=jnp.int32)[:, None] == slot_of[None, :]).astype(
        jnp.int32
    )
    filled = jnp.sum(slot_match, axis=1)
    slot_pair = jnp.sum(slot_match * jnp.arange(pair_count, dtype=jnp.int32)[None, :], axis=1)
    slot_target = jnp.where(filled > 0, pair_target[slot_pair], -1)
    keep_slot = filled.astype(jnp.bfloat16)[:, None, None]
    computed = translate(trans_table, pair_class, block_data[pair_source])
    outgoing = computed[slot_pair] * keep_slot
    outgoing = outgoing.reshape(devices, capacity, 2 * mode_count, columns)
    arrived = lax.all_to_all(outgoing, "sph", split_axis=0, concat_axis=0, tiled=True)
    targets = lax.all_to_all(
        slot_target.reshape(devices, capacity), "sph", split_axis=0, concat_axis=0, tiled=True
    ).reshape(slot_count)
    partial_value = arrived.reshape(slot_count, 2 * mode_count, columns)
    gather_matrix = (jnp.arange(block_count, dtype=jnp.int32)[:, None] == targets[None, :]).astype(
        jnp.bfloat16
    )
    summed = jnp.dot(
        gather_matrix,
        partial_value.reshape(slot_count, 2 * mode_count * columns),
        preferred_element_type=jnp.float32,
    )
    summed = (
        summed.reshape(block_count, 2 * mode_count, columns)
        .transpose(1, 0, 2)
        .reshape(2 * mode_count, spheres, directions)
    )
    total_real = inc_real + summed[:mode_count]
    total_imag = inc_imag + summed[mode_count:]
    out_real = mie_real * total_real - mie_imag * total_imag
    out_imag = mie_real * total_imag + mie_imag * total_real
    scattered = (
        jnp.concatenate([out_real, out_imag], 0)
        .reshape(2 * mode_count, spheres * directions)
        .astype(jnp.bfloat16)
    )
    local_ext = jnp.sum(inc_real * out_real + inc_imag * out_imag, axis=(0, 1))
    extinction = lax.psum(local_ext, "sph")
    return (scattered, extinction)


def solution(mesh):
    placed = (
        P("sph", None),
        P(),
        P(),
        P("groups"),
        P(None, None, "sph"),
        P(),
        P("sph", None),
        P("sph"),
        P("sph"),
        P("sph"),
    )
    return jax.shard_map(
        shards,
        mesh=mesh,
        in_specs=placed,
        out_specs=(P(None, ("groups", "sph")), P("groups")),
        check_vma=False,
    )
```

profile of v0, /device:TPU:0, one launch (start us, length us, event | category | flops | bytes accessed | tf_op | source)
XLA Modules:
  0.0 671.2 jit_solution(2450275542576880069)
XLA Ops:
  5.5 7.4 %all-to-all-start = ((s32[16,1,8]{2,1,0:T(1,128)}), s32[16,1,8]{2,1,0:T(1,128)S(1)}, u32[]{:S(2)}, u32[]{:S(2)}) async-start(s32[16,1,8]{2,1,0:T(1,128)} %bitcast.24), calls=%async_computation | async-start | bytes 16384 | tf_op jit(solution)/shard_map/all_to_all | solution.py:97
  21.9 4.3 gather_fusion.2
  26.3 134.5 %while.10 = (s32[]{:T(128)}, bf16[8,8,896,64]{2,3,1,0:T(8,128)(2,1)}, s32[8,8]{1,0:T(8,128)S(1)}, bf16[8,2,448,448]{3,2,1,0:T(8,128)(2,1)}, bf16[8,8,896,64]{2,3,1,0:T(8,128)(2,1)}, /*index=5*/s32[]{:T(128)}) while((s32[]{:T(128)}, bf16[8,8,896,64]{2,3,1,0:T(8,128)(2,1)}, s32[8,8]{1,0:T(8,128)S(1)}, bf16[8,2,448,448]{3,2,1,0:T(8,128)(2,1)}, ...), condition=%wide.region_5.6_spmd, body=%wide.region_4.5_spmd.sunk | while | flops 824837120 | bytes 63836904 | solution.py:48
  26.3 7.0 %gather_fusion = bf16[8,2,448,448]{3,2,1,0:T(8,128)(2,1)} fusion(bf16[8,2,448,448]{3,2,1,0:T(8,128)(2,1)} %get-tuple-element.133, s32[1024]{0:T(1024)S(1)} %pad_clamp_fusion.4), kind=kCustom, calls=%fused_computation.clone.1 | custom fusion | bytes 12845088 | tf_op jit(solution)/shard_map/while/body/eval_jaxpr/gather | solution.py:37
  43.1 7.0 %gather_fusion = bf16[8,2,448,448]{3,2,1,0:T(8,128)(2,1)} fusion(bf16[8,2,448,448]{3,2,1,0:T(8,128)(2,1)} %get-tuple-element.133, s32[1024]{0:T(1024)S(1)} %pad_clamp_fusion.4), kind=kCustom, calls=%fused_computation.clone.1 | custom fusion | bytes 12845088 | tf_op jit(solution)/shard_map/while/body/eval_jaxpr/gather | solution.py:37
  51.5 3.5 fusion.68
  59.9 7.0 %gather_fusion = bf16[8,2,448,448]{3,2,1,0:T(8,128)(2,1)} fusion(bf16[8,2,448,448]{3,2,1,0:T(8,128)(2,1)} %get-tuple-element.133, s32[1024]{0:T(1024)S(1)} %pad_clamp_fusion.4), kind=kCustom, calls=%fused_computation.clone.1 | custom fusion | bytes 12845088 | tf_op jit(solution)/shard_map/while/body/eval_jaxpr/gather | solution.py:37
  68.3 3.5 fusion.68
  76.7 7.0 %gather_fusion = bf16[8,2,448,448]{3,2,1,0:T(8,128)(2,1)} fusion(bf16[8,2,448,448]{3,2,1,0:T(8,128)(2,1)} %get-tuple-element.133, s32[1024]{0:T(1024)S(1)} %pad_clamp_fusion.4), kind=kCustom, calls=%fused_computation.clone.1 | custom fusion | bytes 12845088 | tf_op jit(solution)/shard_map/while/body/eval_jaxpr/gather | solution.py:37
  93.5 7.0 %gather_fusion = bf16[8,2,448,448]{3,2,1,0:T(8,128)(2,1)} fusion(bf16[8,2,448,448]{3,2,1,0:T(8,128)(2,1)} %get-tuple-element.133, s32[1024]{0:T(1024)S(1)} %pad_clamp_fusion.4), kind=kCustom, calls=%fused_computation.clone.1 | custom fusion | bytes 12845088 | tf_op jit(solution)/shard_map/while/body/eval_jaxpr/gather | solution.py:37
  101.9 3.5 fusion.68
  110.3 7.0 %gather_fusion = bf16[8,2,448,448]{3,2,1,0:T(8,128)(2,1)} fusion(bf16[8,2,448,448]{3,2,1,0:T(8,128)(2,1)} %get-tuple-element.133, s32[1024]{0:T(1024)S(1)} %pad_clamp_fusion.4), kind=kCustom, calls=%fused_computation.clone.1 | custom fusion | bytes 12845088 | tf_op jit(solution)/shard_map/while/body/eval_jaxpr/gather | solution.py:37
  127.1 7.0 %gather_fusion = bf16[8,2,448,448]{3,2,1,0:T(8,128)(2,1)} fusion(bf16[8,2,448,448]{3,2,1,0:T(8,128)(2,1)} %get-tuple-element.133, s32[1024]{0:T(1024)S(1)} %pad_clamp_fusion.4), kind=kCustom, calls=%fused_computation.clone.1 | custom fusion | bytes 12845088 | tf_op jit(solution)/shard_map/while/body/eval_jaxpr/gather | solution.py:37
  144.0 7.0 %gather_fusion = bf16[8,2,448,448]{3,2,1,0:T(8,128)(2,1)} fusion(bf16[8,2,448,448]{3,2,1,0:T(8,128)(2,1)} %get-tuple-element.133, s32[1024]{0:T(1024)S(1)} %pad_clamp_fusion.4), kind=kCustom, calls=%fused_computation.clone.1 | custom fusion | bytes 12845088 | tf_op jit(solution)/shard_map/while/body/eval_jaxpr/gather | solution.py:37
  160.7 12.3 %gather_fusion.3 = bf16[128,896,64]{1,2,0:T(8,128)(2,1)} fusion(bf16[64,896,64]{1,2,0:T(8,128)(2,1)} %bitcast.33, s32[1024]{0:T(1024)S(1)} %pad_clamp_fusion.2), kind=kCustom, calls=%fused_computation.3 | custom fusion | bytes 29360640 | tf_op jit(solution)/shard_map/gather | solution.py:94
  173.1 13.5 %broadcast_multiply_fusion = bf16[16,8,896,64]{2,3,1,0:T(8,128)(2,1)} fusion(bf16[16,8,896,64]{2,3,1,0:T(8,128)(2,1)} %bitcast.236, bf16[16,8]{1,0:T(8,128)(2,1)S(1)} %convert_element_type.32), kind=kLoop, calls=%fused_computation.29 | loop fusion | flops 7340032 | bytes 29360384 | tf_op jit(solution)/shard_map/mul | solution.py:94
  186.6 6.0 all-to-all-start.1
  194.7 258.1 %all-to-all-done.1 = bf16[16,8,896,64]{2,3,1,0:T(8,128)(2,1)} async-done(((bf16[16,8,896,64]{2,3,1,0:T(8,128)(2,1)}), bf16[16,8,896,64]{2,3,1,0:T(8,128)(2,1)}, u32[]{:S(2)}, u32[]{:S(2)}) %all-to-all-start.1) | async-done | bytes 14680096 | tf_op jit(solution)/shard_map/all_to_all | solution.py:96
  452.8 26.5 %copy.80 = bf16[16,8,896,64]{3,2,1,0:T(8,128)(2,1)} copy(bf16[16,8,896,64]{2,3,1,0:T(8,128)(2,1)} %all-to-all-done.1) | data formatting | bytes 29360128 | tf_op jit(solution)/shard_map/all_to_all | solution.py:96
  479.3 28.1 %reshape_reshape.3 = bf16[128,57344]{1,0:T(8,128)(2,1)} reshape(bf16[16,8,896,64]{3,2,1,0:T(8,128)(2,1)} %copy.80) | data formatting | bytes 29360128 | tf_op jit(solution)/shard_map/reshape;reshape | solution.py:106
  507.4 20.2 %copy.81 = bf16[57344,128]{1,0:T(8,128)(2,1)} copy(bf16[57344,128]{0,1:T(8,128)(2,1)} %bitcast.238) | data formatting | bytes 29360128 | tf_op jit(solution)/shard_map/dot_general | solution.py:104
  527.6 35.5 %fusion.34 = f32[896,16,64]{0,1,2:T(8,128)} fusion(bf16[896,64,128]{2,1,0:T(8,128)(2,1)} %bitcast.237, s32[128]{0:T(128)S(1)} %eq.64), kind=kOutput, calls=%fused_computation.61 | convolution fusion | flops 234883072 | bytes 18350592 | tf_op jit(solution)/shard_map/dot_general | solution.py:104
  563.1 9.9 %add_reduce_fusion = (f32[16,64]{0,1:T(8,128)S(1)}, f32[448,16,64]{0,1,2:T(8,128)S(1)}, f32[448,16,64]{0,1,2:T(8,128)S(1)}) fusion(f32[448,16,64]{0,2,1:T(8,128)S(1)} %bitcast.241, f32[448,16,64]{0,2,1:T(8,128)} %bitcast.247, f32[448,16,64]{0,2,1:T(8,128)S(1)} %bitcast.243, f32[448,16,64]{0,2,1:T(8,128)S(1)} %bitcast.245, f32[16,64]{0,1:T(8,128)S(1)} %copy.87, ...), kind=kLoop, calls=%fused_computation.60 | loop fusion | flops 8256512 | bytes 14692352 | tf_op jit(solution)/shard_map/reduce_sum | solution.py:123
  580.4 90.4 %psum.7 = f32[32]{0:T(128)} all-reduce(f32[32]{0:T(128)S(1)} %reduce_sum.51), channel_id=1, replica_groups=mesh['groups'=2,'sph'=16] {'sph'}, use_global_device_ids=true, to_apply=%region_8.9 | all-reduce | flops 32 | bytes 256 | tf_op jit(solution)/shard_map/psum | solution.py:124
  (192 shorter events, 90.8 us)
Async XLA Ops:
  0.6 15.6 %copy-start = (f32[2,448,256]{2,1,0:T(8,128)S(1)}, f32[2,448,256]{2,1,0:T(8,128)}, u32[]{:S(2)}) copy-start(f32[2,448,256]{2,1,0:T(8,128)} %param.14) | copy-start | bytes 2752516
  0.6 16.9 %copy-start.20 = (s32[64]{0:T(128)S(1)}, s32[64]{0:T(128)}, u32[]{:S(2)}) copy-start(s32[64]{0:T(128)} %param.19) | copy-start | bytes 772
  0.7 16.9 %copy-start.19 = (s32[64]{0:T(128)S(1)}, s32[64]{0:T(128)}, u32[]{:S(2)}) copy-start(s32[64]{0:T(128)} %param.21) | copy-start | bytes 772
  0.7 17.0 %copy-start.18 = (f32[2,448,32]{1,2,0:T(8,128)S(1)}, f32[2,448,32]{1,2,0:T(8,128)}, u32[]{:S(2)}) copy-start(f32[2,448,32]{1,2,0:T(8,128)} %param.16) | copy-start | bytes 344068
  5.5 181.1 %all-to-all-start = ((s32[16,1,8]{2,1,0:T(1,128)}), s32[16,1,8]{2,1,0:T(1,128)S(1)}, u32[]{:S(2)}, u32[]{:S(2)}) async-start(s32[16,1,8]{2,1,0:T(1,128)} %bitcast.24), calls=%async_computation | async-start | bytes 16384 | tf_op jit(solution)/shard_map/all_to_all | solution.py:97
  18.0 1.3 copy-start.3
  18.3 1.7 copy-start.5
  18.6 2.5 copy-start.7
  18.9 2.5 copy-start.9
  33.3 4.9 copy-start.2
  50.1 4.9 copy-start.2
  66.9 4.9 copy-start.2
  83.7 4.9 copy-start.2
  100.5 4.9 copy-start.2
  117.3 4.9 copy-start.2
  134.1 4.9 copy-start.2
  151.0 4.9 copy-start.2
  186.6 266.2 %all-to-all-start.1 = ((bf16[16,8,896,64]{2,3,1,0:T(8,128)(2,1)}), bf16[16,8,896,64]{2,3,1,0:T(8,128)(2,1)}, u32[]{:S(2)}, u32[]{:S(2)}) async-start(bf16[16,8,896,64]{2,3,1,0:T(8,128)(2,1)} %broadcast_multiply_fusion), calls=%async_computation.1 | async-start | bytes 29360128 | tf_op jit(solution)/shard_map/all_to_all | solution.py:96
  527.6 35.5 %copy-start.4 = (f32[448,32,32]{0,2,1:T(8,128)S(1)}, f32[448,32,32]{0,2,1:T(8,128)}, u32[]{:S(2)}) copy-start(f32[448,32,32]{0,2,1:T(8,128)} %copy-done.3) | copy-start | bytes 5505028
  527.6 35.5 %copy-start.6 = (f32[448,32,32]{0,2,1:T(8,128)S(1)}, f32[448,32,32]{0,2,1:T(8,128)}, u32[]{:S(2)}) copy-start(f32[448,32,32]{0,2,1:T(8,128)} %copy-done.5) | copy-start | bytes 5505028
  527.6 35.5 %copy-start.8 = (f32[448,32,32]{0,2,1:T(8,128)S(1)}, f32[448,32,32]{0,2,1:T(8,128)}, u32[]{:S(2)}) copy-start(f32[448,32,32]{0,2,1:T(8,128)} %copy-done.7) | copy-start | bytes 5505028
  574.3 1.3 copy-start.11
  574.3 1.3 copy-start.13
  577.2 93.6 %copy-start.1 = (f32[2,448,256]{2,1,0:T(8,128)S(1)}, f32[2,448,256]{2,1,0:T(8,128)}, u32[]{:S(2)}) copy-start(f32[2,448,256]{2,1,0:T(8,128)} %param.14) | copy-start | bytes 2752516
  (6 other events, 5.3 us)
where the time goes:
time: 683 us; the launch traced here: 671 us
  waiting for transfers between devices  258 us (38%)
  local copies, waits for them, and re-layouts  172 us (25%)
  matrix products  94.1 us (14%)
  blocking collectives  90.4 us (13%)
  other arithmetic  41 us (6%)
  starting transfers between devices  13.5 us (2%)
    all_to_all x1, waiting for transfers between devices, shards(): lax.all_to_all(outgoing, 'sph', split_axis=0, concat_axis=0, tiled=True)  258 us
    psum x1, blocking collectives, shards(): extinction = lax.psum(local_ext, 'sph')  90.4 us
    gather x8, local copies, waits for them, and re-layouts, one_group(): tables = trans_table[picked]  56.2 us
    dot_general x1, matrix products, shards(): jnp.dot(gather_matrix, partial_value.reshape(slot_count, 2 * mode_count *...  35.5 us
    another operation x1, local copies, waits for them, and re-layouts, shards(): partial_value.reshape(slot_count, 2 * mode_count * columns)  28.1 us
    dot_general x8, matrix products, one_group(): jnp.einsum('kij,kjc->kic', tables[:, 0], data_real, preferred_element_typ...  27.6 us
    all_to_all x1, local copies, waits for them, and re-layouts, shards(): lax.all_to_all(outgoing, 'sph', split_axis=0, concat_axis=0, tiled=True)  26.5 us
    dot_general x1, local copies, waits for them, and re-layouts, shards(): jnp.dot(gather_matrix, partial_value.reshape(slot_count, 2 * mode_count *...  20.2 us
  transfers between devices with their start and end apart: 2, of which 1 were waited for; matrix products, arithmetic and copies ran while one was open for 26% of the time, Pallas kernels for 0%

commit v1 on v0

--- a/solution.py
+++ b/solution.py
@@ -5,6 +5,29 @@
 
 BLOCK = 2
 HIGHEST_PRECISION = lax.Precision.HIGHEST
+
+
+def cut_along(value, dim, devices):
+    shape = value.shape
+    blocks = value.reshape(*shape[:dim], devices, shape[dim] // devices, *shape[dim + 1 :])
+    return jnp.moveaxis(blocks, dim, 0)
+
+
+def in_order(tiles, dim):
+    lengths = list(tiles.shape[1:])
+    lengths[dim] *= tiles.shape[0]
+    return jnp.moveaxis(tiles, 0, dim).reshape(lengths)
+
+
+def exchange_in_pairs(x, axis, split_dim, concat_dim):
+    length, mine = (lax.axis_size(axis), lax.axis_index(axis))
+    pieces = cut_along(x, split_dim, length)
+    done = [pieces[mine]]
+    for hop in range(1, length):
+        sent = pieces[mine ^ hop]
+        done.append(lax.ppermute(sent, axis, [(i, i ^ hop) for i in range(length)]))
+    pieces = jnp.stack(done)[mine ^ jnp.arange(length)]
+    return in_order(pieces, concat_dim)
 
 
 def incident_field(positions, wave_vectors, pattern, dir_index):
@@ -93,7 +116,7 @@
     computed = translate(trans_table, pair_class, block_data[pair_source])
     outgoing = computed[slot_pair] * keep_slot
     outgoing = outgoing.reshape(devices, capacity, 2 * mode_count, columns)
-    arrived = lax.all_to_all(outgoing, "sph", split_axis=0, concat_axis=0, tiled=True)
+    arrived = exchange_in_pairs(outgoing, "sph", 0, 0)
     targets = lax.all_to_all(
         slot_target.reshape(devices, capacity), "sph", split_axis=0, concat_axis=0, tiled=True
     ).reshape(slot_count)

time: 683 us -> 753 us (1.10)
  local copies, waits for them, and re-layouts: 172 us -> 216 us
  starting transfers between devices: 13.5 us -> 25.4 us
  matrix products: 94.1 us -> 103 us
  blocking collectives: 90.4 us -> 98.9 us
    all_to_all x1 -> x0, waiting for transfers between devices: 258 us -> none  [shards(): lax.all_to_all(outgoing, 'sph', split_axis=0, concat_axis=0, tiled=True)]
    ppermute x0 -> x15, waiting for transfers between devices: none -> 220 us  [exchange_in_pairs(): done.append(lax.ppermute(sent, axis, [(i, i ^ hop) for i in range(length)]))]
    gather x0 -> x2, local copies, waits for them, and re-layouts: none -> 39.4 us  [exchange_in_pairs(): pieces = jnp.stack(done)[mine ^ jnp.arange(length)]]
    all_to_all x1, waiting for transfers between devices: 0.01 us -> 36.2 us  [shards(): lax.all_to_all(slot_target.reshape(devices, capacity), 'sph', split_axis=...]
    all_to_all x1 -> x0, local copies, waits for them, and re-layouts: 26.5 us -> none  [shards(): lax.all_to_all(outgoing, 'sph', split_axis=0, concat_axis=0, tiled=True)]
    ppermute x0 -> x15, starting transfers between devices: none -> 19 us  [exchange_in_pairs(): done.append(lax.ppermute(sent, axis, [(i, i ^ hop) for i in range(length)]))]
    unnamed x41 -> x67, local copies, waits for them, and re-layouts: 3.94 us -> 20.8 us
    squeeze x0 -> x1, local copies, waits for them, and re-layouts: none -> 10.8 us  [exchange_in_pairs(): sent = pieces[mine ^ hop]]
  transfers between devices with their start and end apart: 2 -> 16, of which waited for: 1 -> 6; matrix products, arithmetic and copies ran while one was open for 26% -> 3% of each run, Pallas kernels for 0% -> 0%
where the time goes in v1:
time: 753 us; the launch traced here: 743 us
  waiting for transfers between devices  256 us (34%)
  local copies, waits for them, and re-layouts  216 us (29%)
  matrix products  103 us (14%)
  blocking collectives  98.9 us (13%)
  other arithmetic  41.6 us (6%)
  starting transfers between devices  25.4 us (3%)
    ppermute x15, waiting for transfers between devices, exchange_in_pairs(): done.append(lax.ppermute(sent, axis, [(i, i ^ hop) for i in range(length)]))  220 us
    psum x1, blocking collectives, shards(): extinction = lax.psum(local_ext, 'sph')  98.9 us
    gather x8, local copies, waits for them, and re-layouts, one_group(): tables = trans_table[picked]  57 us
    dot_general x1, matrix products, shards(): jnp.dot(gather_matrix, partial_value.reshape(slot_count, 2 * mode_count *...  44 us
    gather x2, local copies, waits for them, and re-layouts, exchange_in_pairs(): pieces = jnp.stack(done)[mine ^ jnp.arange(length)]  39.4 us
    all_to_all x1, waiting for transfers between devices, shards(): lax.all_to_all(slot_target.reshape(devices, capacity), 'sph', split_axis=...  36.2 us
    another operation x1, local copies, waits for them, and re-layouts, shards(): partial_value.reshape(slot_count, 2 * mode_count * columns)  28.1 us
    dot_general x8, matrix products, one_group(): jnp.einsum('kij,kjc->kic', tables[:, 0], data_real, preferred_element_typ...  27.6 us
  transfers between devices with their start and end apart: 16, of which 6 were waited for; matrix products, arithmetic and copies ran while one was open for 3% of the time, Pallas kernels for 0%

profile of v1, /device:TPU:0, one launch (start us, length us, event | category | flops | bytes accessed | tf_op | source)
XLA Modules:
  0.0 742.5 jit_solution(17099365467838386566)
XLA Ops:
  18.6 135.3 %while.10 = (s32[]{:T(128)}, bf16[8,8,896,64]{2,3,1,0:T(8,128)(2,1)}, s32[8,8]{1,0:T(8,128)S(1)}, bf16[8,2,448,448]{3,2,1,0:T(8,128)(2,1)}, bf16[8,8,896,64]{2,3,1,0:T(8,128)(2,1)}, /*index=5*/s32[]{:T(128)}) while((s32[]{:T(128)}, bf16[8,8,896,64]{2,3,1,0:T(8,128)(2,1)}, s32[8,8]{1,0:T(8,128)S(1)}, bf16[8,2,448,448]{3,2,1,0:T(8,128)(2,1)}, ...), condition=%wide.region_5.6_spmd, body=%wide.region_4.5_spmd.sunk | while | flops 824837120 | bytes 63836904 | solution.py:71
  18.6 7.1 gather_fusion
  35.5 7.1 gather_fusion
  52.4 7.1 gather_fusion
  69.4 7.1 gather_fusion
  86.3 7.1 gather_fusion
  120.1 7.1 gather_fusion
  137.0 7.1 gather_fusion
  154.0 12.3 %gather_fusion.3 = bf16[128,896,64]{1,2,0:T(8,128)(2,1)} fusion(bf16[64,896,64]{1,2,0:T(8,128)(2,1)} %bitcast.33, s32[1024]{0:T(1024)S(1)} %get-tuple-element.104), kind=kCustom, calls=%fused_computation.3 | custom fusion | bytes 29360640 | tf_op jit(solution)/shard_map/gather | solution.py:117
  167.6 13.5 %broadcast_multiply_fusion = bf16[16,1,8,896,64]{3,4,2,0,1:T(8,128)(2,1)} fusion(bf16[16,1,8,896,64]{3,4,2,0,1:T(8,128)(2,1)} %bitcast.299, bf16[16,8]{1,0:T(8,128)(2,1)S(1)} %convert_element_type.32), kind=kLoop, calls=%fused_computation.30 | loop fusion | flops 7340032 | bytes 29360384 | tf_op jit(solution)/shard_map/mul | solution.py:117
  181.1 10.8 %dynamic-slice_bitcast_fusion.1 = (bf16[1,8,896,64]{2,3,1,0:T(8,128)(2,1)}, bf16[1,8,896,64]{2,3,1,0:T(8,128)(2,1)}, bf16[1,8,896,64]{2,3,1,0:T(8,128)(2,1)}, bf...) fusion(bf16[16,1,8,896,64]{3,4,2,0,1:T(8,128)(2,1)} %broadcast_, ...), kind=kLoop, calls=%fused_computation.81 | loop fusion | bytes 29360192 | tf_op jit(solution)/shard_map/squeeze | solution.py:27
  204.8 36.2 %all-to-all-done = s32[16,1,8]{2,1,0:T(1,128)S(1)} async-done(((s32[16,1,8]{2,1,0:T(1,128)}), s32[16,1,8]{2,1,0:T(1,128)S(1)}, u32[]{:S(2)}, u32[]{:S(2)}) %all-to-all-start) | async-done | bytes 544 | tf_op jit(solution)/shard_map/all_to_all | solution.py:120
  255.9 42.6 %collective-permute-done.5 = bf16[1,8,896,64]{2,3,1,0:T(8,128)(2,1)S(1)} collective-permute-done((bf16[1,8,896,64]{2,3,1,0:T(8,128)(2,1)}, bf16[1,8,896,64]{2,3,1,0:T(8,128)(2,1)S(1)}, u32[]{:S(2)}, u32[]{:S(2)}) %collective-permute-start.5) | collective-permute-done | bytes 917536 | tf_op jit(solution)/shard_map/ppermute | solution.py:28
  299.5 16.3 %collective-permute-done.6 = bf16[1,8,896,64]{2,3,1,0:T(8,128)(2,1)S(1)} collective-permute-done((bf16[1,8,896,64]{2,3,1,0:T(8,128)(2,1)}, bf16[1,8,896,64]{2,3,1,0:T(8,128)(2,1)S(1)}, u32[]{:S(2)}, u32[]{:S(2)}) %collective-permute-start.6) | collective-permute-done | bytes 917536 | tf_op jit(solution)/shard_map/ppermute | solution.py:28
  322.3 88.4 %collective-permute-done.8 = bf16[1,8,896,64]{2,3,1,0:T(8,128)(2,1)S(1)} collective-permute-done((bf16[1,8,896,64]{2,3,1,0:T(8,128)(2,1)S(1)}, bf16[1,8,896,64]{2,3,1,0:T(8,128)(2,1)S(1)}, u32[]{:S(2)}, u32[]{:S(2)}) %collective-permute-start.8) | collective-permute-done | bytes 917536 | tf_op jit(solution)/shard_map/ppermute | solution.py:28
  413.2 36.9 %collective-permute-done.9 = bf16[1,8,896,64]{2,3,1,0:T(8,128)(2,1)S(1)} collective-permute-done((bf16[1,8,896,64]{2,3,1,0:T(8,128)(2,1)S(1)}, bf16[1,8,896,64]{2,3,1,0:T(8,128)(2,1)S(1)}, u32[]{:S(2)}, u32[]{:S(2)}) %collective-permute-start.9) | collective-permute-done | bytes 917536 | tf_op jit(solution)/shard_map/ppermute | solution.py:28
  453.3 36.0 %collective-permute-done.10 = bf16[1,8,896,64]{2,3,1,0:T(8,128)(2,1)S(1)} collective-permute-done((bf16[1,8,896,64]{2,3,1,0:T(8,128)(2,1)S(1)}, bf16[1,8,896,64]{2,3,1,0:T(8,128)(2,1)S(1)}, u32[]{:S(2)}, u32[]{:S(2)}) %collective-permute-start.10) | collective-permute-done | bytes 917536 | tf_op jit(solution)/shard_map/ppermute | solution.py:28
  494.5 12.8 %gather_fusion.4 = bf16[16,8,896,64]{2,3,1,0:T(8,128)(2,1)} fusion(bf16[16,8,896,64]{2,3,1,0:T(8,128)(2,1)} %bitcast.300, s32[1024]{0:T(1024)S(1)} %pad_clamp_fusion.1), kind=kCustom, calls=%fused_computation.4 | custom fusion | bytes 29360192 | tf_op jit(solution)/shard_map/gather | solution.py:29
  507.2 26.6 %copy.97 = bf16[16,8,896,64]{3,2,1,0:T(8,128)(2,1)} copy(bf16[16,8,896,64]{2,3,1,0:T(8,128)(2,1)} %gather_fusion.4) | data formatting | bytes 29360128 | tf_op jit(solution)/shard_map/gather | solution.py:29
  533.8 28.1 %reshape_reshape_reshape.3 = bf16[128,57344]{1,0:T(8,128)(2,1)} reshape(bf16[16,8,896,64]{3,2,1,0:T(8,128)(2,1)} %copy.97) | data formatting | bytes 29360128 | tf_op jit(solution)/shard_map/reshape;reshape;reshape | solution.py:129
  562.0 19.9 %copy.98 = bf16[57344,128]{1,0:T(8,128)(2,1)} copy(bf16[57344,128]{0,1:T(8,128)(2,1)} %bitcast.302) | data formatting | bytes 29360128 | tf_op jit(solution)/shard_map/dot_general | solution.py:127
  581.9 44.0 %fusion.34 = f32[896,16,64]{0,1,2:T(8,128)} fusion(bf16[896,64,128]{2,1,0:T(8,128)(2,1)} %bitcast.301, s32[128]{0:T(128)S(1)} %eq.64), kind=kOutput, calls=%fused_computation.62 | convolution fusion | flops 234883072 | bytes 18350592 | tf_op jit(solution)/shard_map/dot_general | solution.py:127
  625.9 9.9 %add_reduce_fusion = (f32[16,64]{0,1:T(8,128)S(1)}, f32[448,16,64]{0,1,2:T(8,128)S(1)}, f32[448,16,64]{0,1,2:T(8,128)S(1)}) fusion(f32[448,16,64]{0,2,1:T(8,128)S(1)} %bitcast.305, f32[448,16,64]{0,2,1:T(8,128)} %bitcast.311, f32[448,16,64]{0,2,1:T(8,128)S(1)} %bitcast.307, f32[448,16,64]{0,2,1:T(8,128)S(1)} %bitcast.309, f32[16,64]{0,1:T(8,128)S(1)} %copy.104, ...), kind=kLoop, calls=%fused_computation.61 | loop fusion | flops 8256512 | bytes 14692352 | tf_op jit(solution)/shard_map/reduce_sum | solution.py:146
  643.2 98.9 %psum.7 = f32[32]{0:T(128)} all-reduce(f32[32]{0:T(128)S(1)} %reduce_sum.51), channel_id=1, replica_groups=mesh['groups'=2,'sph'=16] {'sph'}, use_global_device_ids=true, to_apply=%region_8.9 | all-reduce | flops 32 | bytes 256 | tf_op jit(solution)/shard_map/psum | solution.py:147
  (250 shorter events, 157.6 us)
Async XLA Ops:
  191.9 50.3 %collective-permute-start = (bf16[1,8,896,64]{2,3,1,0:T(8,128)(2,1)}, bf16[1,8,896,64]{2,3,1,0:T(8,128)(2,1)}, u32[]{:S(2)}, u32[]{:S(2)}) collective-permute-start(bf16[1,8,896,64]{2,3,1,0:T(8,128)(2,1)} %get-tuple-element.80), channel_id=1, source_target_pairs={{0,1},{1,0},{2,3},{3,2},{4,5},{5,4},{6,7},{7,6},{8,9},{9,8},{10,11... | collective-permute-start | bytes 2752520 | tf_op jit(solution)/shard_map/ppermute | solution.py:28
  192.5 52.7 %collective-permute-start.1 = (bf16[1,8,896,64]{2,3,1,0:T(8,128)(2,1)}, bf16[1,8,896,64]{2,3,1,0:T(8,128)(2,1)}, u32[]{:S(2)}, u32[]{:S(2)}) collective-permute-start(bf16[1,8,896,64]{2,3,1,0:T(8,128)(2,1)} %get-tuple-element.79), channel_id=1, source_target_pairs={{0,2},{1,3},{2,0},{3,1},{4,6},{5,7},{6,4},{7,5},{8,10},{9,11},{10,... | collective-permute-start | bytes 2752520 | tf_op jit(solution)/shard_map/ppermute | solution.py:28
  195.1 53.8 %collective-permute-start.2 = (bf16[1,8,896,64]{2,3,1,0:T(8,128)(2,1)}, bf16[1,8,896,64]{2,3,1,0:T(8,128)(2,1)S(1)}, u32[]{:S(2)}, u32[]{:S(2)}) collective-permute-start(bf16[1,8,896,64]{2,3,1,0:T(8,128)(2,1)} %get-tuple-element.78), channel_id=1, source_target_pairs={{0,3},{1,2},{2,1},{3,0},{4,7},{5,6},{6,5},{7,4},{8,11},{9,10},{10,... | collective-permute-start | bytes 2752520 | tf_op jit(solution)/shard_map/ppermute | solution.py:28
  195.1 55.4 %collective-permute-start.3 = (bf16[1,8,896,64]{2,3,1,0:T(8,128)(2,1)}, bf16[1,8,896,64]{2,3,1,0:T(8,128)(2,1)S(1)}, u32[]{:S(2)}, u32[]{:S(2)}) collective-permute-start(bf16[1,8,896,64]{2,3,1,0:T(8,128)(2,1)} %get-tuple-element.77), channel_id=1, source_target_pairs={{0,4},{1,5},{2,6},{3,7},{4,0},{5,1},{6,2},{7,3},{8,12},{9,13},{10,... | collective-permute-start | bytes 2752520 | tf_op jit(solution)/shard_map/ppermute | solution.py:28
  196.9 57.4 %collective-permute-start.4 = (bf16[1,8,896,64]{2,3,1,0:T(8,128)(2,1)}, bf16[1,8,896,64]{2,3,1,0:T(8,128)(2,1)S(1)}, u32[]{:S(2)}, u32[]{:S(2)}) collective-permute-start(bf16[1,8,896,64]{2,3,1,0:T(8,128)(2,1)} %get-tuple-element.76), channel_id=1, source_target_pairs={{0,5},{1,4},{2,7},{3,6},{4,1},{5,0},{6,3},{7,2},{8,13},{9,12},{10,... | collective-permute-start | bytes 2752520 | tf_op jit(solution)/shard_map/ppermute | solution.py:28
  197.6 43.4 %all-to-all-start = ((s32[16,1,8]{2,1,0:T(1,128)}), s32[16,1,8]{2,1,0:T(1,128)S(1)}, u32[]{:S(2)}, u32[]{:S(2)}) async-start(s32[16,1,8]{2,1,0:T(1,128)} %bitcast.24), calls=%async_computation | async-start | bytes 16384 | tf_op jit(solution)/shard_map/all_to_all | solution.py:120
  242.2 56.2 %collective-permute-start.5 = (bf16[1,8,896,64]{2,3,1,0:T(8,128)(2,1)}, bf16[1,8,896,64]{2,3,1,0:T(8,128)(2,1)S(1)}, u32[]{:S(2)}, u32[]{:S(2)}) collective-permute-start(bf16[1,8,896,64]{2,3,1,0:T(8,128)(2,1)} %get-tuple-element.75), channel_id=1, source_target_pairs={{0,6},{1,7},{2,4},{3,5},{4,2},{5,3},{6,0},{7,1},{8,14},{9,15},{10,... | collective-permute-start | bytes 2752520 | tf_op jit(solution)/shard_map/ppermute | solution.py:28
  245.1 53.3 %copy-start.15 = (bf16[1,8,896,64]{2,3,1,0:T(8,128)(2,1)S(1)}, bf16[1,8,896,64]{2,3,1,0:T(8,128)(2,1)}, u32[]{:S(2)}) copy-start(bf16[1,8,896,64]{2,3,1,0:T(8,128)(2,1)} %get-tuple-element.70) | copy-start | bytes 2752516
  245.1 70.6 %collective-permute-start.6 = (bf16[1,8,896,64]{2,3,1,0:T(8,128)(2,1)}, bf16[1,8,896,64]{2,3,1,0:T(8,128)(2,1)S(1)}, u32[]{:S(2)}, u32[]{:S(2)}) collective-permute-start(bf16[1,8,896,64]{2,3,1,0:T(8,128)(2,1)} %get-tuple-element.74), channel_id=1, source_target_pairs={{0,7},{1,6},{2,5},{3,4},{4,3},{5,2},{6,1},{7,0},{8,15},{9,14},{10,... | collective-permute-start | bytes 2752520 | tf_op jit(solution)/shard_map/ppermute | solution.py:28
  248.9 66.9 %copy-start.14 = (bf16[1,8,896,64]{2,3,1,0:T(8,128)(2,1)S(1)}, bf16[1,8,896,64]{2,3,1,0:T(8,128)(2,1)}, u32[]{:S(2)}) copy-start(bf16[1,8,896,64]{2,3,1,0:T(8,128)(2,1)} %get-tuple-element.69) | copy-start | bytes 2752516
  248.9 70.3 %collective-permute-start.7 = (bf16[1,8,896,64]{2,3,1,0:T(8,128)(2,1)S(1)}, bf16[1,8,896,64]{2,3,1,0:T(8,128)(2,1)S(1)}, u32[]{:S(2)}, u32[]{:S(2)}) collective-permute-start(bf16[1,8,896,64]{2,3,1,0:T(8,128)(2,1)S(1)} %copy-done.18), channel_id=1, source_target_pairs={{0,8},{1,9},{2,10},{3,11},{4,12},{5,13},{6,14},{7,15},{8,0},{9,1},... | collective-permute-start | bytes 2752520 | tf_op jit(solution)/shard_map/ppermute | solution.py:28
  250.5 68.6 %copy-start.13 = (bf16[1,8,896,64]{2,3,1,0:T(8,128)(2,1)S(1)}, bf16[1,8,896,64]{2,3,1,0:T(8,128)(2,1)}, u32[]{:S(2)}) copy-start(bf16[1,8,896,64]{2,3,1,0:T(8,128)(2,1)} %get-tuple-element.68) | copy-start | bytes 2752516
  250.5 160.2 %collective-permute-start.8 = (bf16[1,8,896,64]{2,3,1,0:T(8,128)(2,1)S(1)}, bf16[1,8,896,64]{2,3,1,0:T(8,128)(2,1)S(1)}, u32[]{:S(2)}, u32[]{:S(2)}) collective-permute-start(bf16[1,8,896,64]{2,3,1,0:T(8,128)(2,1)S(1)} %copy-done.17), channel_id=1, source_target_pairs={{0,9},{1,8},{2,11},{3,10},{4,13},{5,12},{6,15},{7,14},{8,1},{9,0},... | collective-permute-start | bytes 2752520 | tf_op jit(solution)/shard_map/ppermute | solution.py:28
  254.3 156.5 %copy-start.12 = (bf16[1,8,896,64]{2,3,1,0:T(8,128)(2,1)S(1)}, bf16[1,8,896,64]{2,3,1,0:T(8,128)(2,1)}, u32[]{:S(2)}) copy-start(bf16[1,8,896,64]{2,3,1,0:T(8,128)(2,1)} %get-tuple-element.67) | copy-start | bytes 2752516
  254.3 195.8 %collective-permute-start.9 = (bf16[1,8,896,64]{2,3,1,0:T(8,128)(2,1)S(1)}, bf16[1,8,896,64]{2,3,1,0:T(8,128)(2,1)S(1)}, u32[]{:S(2)}, u32[]{:S(2)}) collective-permute-start(bf16[1,8,896,64]{2,3,1,0:T(8,128)(2,1)S(1)} %copy-done.16), channel_id=1, source_target_pairs={{0,10},{1,11},{2,8},{3,9},{4,14},{5,15},{6,12},{7,13},{8,2},{9,3},... | collective-permute-start | bytes 2752520 | tf_op jit(solution)/shard_map/ppermute | solution.py:28
  298.5 151.6 %copy-start.11 = (bf16[1,8,896,64]{2,3,1,0:T(8,128)(2,1)S(1)}, bf16[1,8,896,64]{2,3,1,0:T(8,128)(2,1)}, u32[]{:S(2)}) copy-start(bf16[1,8,896,64]{2,3,1,0:T(8,128)(2,1)} %get-tuple-element.66) | copy-start | bytes 2752516
  298.5 190.8 %collective-permute-start.10 = (bf16[1,8,896,64]{2,3,1,0:T(8,128)(2,1)S(1)}, bf16[1,8,896,64]{2,3,1,0:T(8,128)(2,1)S(1)}, u32[]{:S(2)}, u32[]{:S(2)}) collective-permute-start(bf16[1,8,896,64]{2,3,1,0:T(8,128)(2,1)S(1)} %copy-done.15), channel_id=1, source_target_pairs={{0,11},{1,10},{2,9},{3,8},{4,15},{5,14},{6,13},{7,12},{8,3},{9,2},... | collective-permute-start | bytes 2752520 | tf_op jit(solution)/shard_map/ppermute | solution.py:28
  315.8 174.5 %collective-permute-start.11 = (bf16[1,8,896,64]{2,3,1,0:T(8,128)(2,1)S(1)}, bf16[1,8,896,64]{2,3,1,0:T(8,128)(2,1)S(1)}, u32[]{:S(2)}, u32[]{:S(2)}) collective-permute-start(bf16[1,8,896,64]{2,3,1,0:T(8,128)(2,1)S(1)} %copy-done.14), channel_id=1, source_target_pairs={{0,12},{1,13},{2,14},{3,15},{4,8},{5,9},{6,10},{7,11},{8,4},{9,5},... | collective-permute-start | bytes 2752520 | tf_op jit(solution)/shard_map/ppermute | solution.py:28
  319.2 172.2 %collective-permute-start.12 = (bf16[1,8,896,64]{2,3,1,0:T(8,128)(2,1)S(1)}, bf16[1,8,896,64]{2,3,1,0:T(8,128)(2,1)S(1)}, u32[]{:S(2)}, u32[]{:S(2)}) collective-permute-start(bf16[1,8,896,64]{2,3,1,0:T(8,128)(2,1)S(1)} %copy-done.13), channel_id=1, source_target_pairs={{0,13},{1,12},{2,15},{3,14},{4,9},{5,8},{6,11},{7,10},{8,5},{9,4},... | collective-permute-start | bytes 2752520 | tf_op jit(solution)/shard_map/ppermute | solution.py:28
  410.8 81.6 %collective-permute-start.13 = (bf16[1,8,896,64]{2,3,1,0:T(8,128)(2,1)S(1)}, bf16[1,8,896,64]{2,3,1,0:T(8,128)(2,1)S(1)}, u32[]{:S(2)}, u32[]{:S(2)}) collective-permute-start(bf16[1,8,896,64]{2,3,1,0:T(8,128)(2,1)S(1)} %copy-done.12), channel_id=1, source_target_pairs={{0,14},{1,15},{2,12},{3,13},{4,10},{5,11},{6,8},{7,9},{8,6},{9,7},... | collective-permute-start | bytes 2752520 | tf_op jit(solution)/shard_map/ppermute | solution.py:28
  450.1 43.3 %collective-permute-start.14 = (bf16[1,8,896,64]{2,3,1,0:T(8,128)(2,1)S(1)}, bf16[1,8,896,64]{2,3,1,0:T(8,128)(2,1)S(1)}, u32[]{:S(2)}, u32[]{:S(2)}) collective-permute-start(bf16[1,8,896,64]{2,3,1,0:T(8,128)(2,1)S(1)} %copy-done.11), channel_id=1, source_target_pairs={{0,15},{1,14},{2,13},{3,12},{4,11},{5,10},{6,9},{7,8},{8,7},{9,6},... | collective-permute-start | bytes 2752520 | tf_op jit(solution)/shard_map/ppermute | solution.py:28
  581.9 44.0 %copy-start.7 = (f32[448,32,32]{0,2,1:T(8,128)S(1)}, f32[448,32,32]{0,2,1:T(8,128)}, u32[]{:S(2)}) copy-start(f32[448,32,32]{0,2,1:T(8,128)} %copy-done.6) | copy-start | bytes 5505028
  581.9 44.0 %copy-start.9 = (f32[448,32,32]{0,2,1:T(8,128)S(1)}, f32[448,32,32]{0,2,1:T(8,128)}, u32[]{:S(2)}) copy-start(f32[448,32,32]{0,2,1:T(8,128)} %copy-done.8) | copy-start | bytes 5505028
  640.0 102.1 %copy-start.1 = (f32[2,448,256]{2,1,0:T(8,128)S(1)}, f32[2,448,256]{2,1,0:T(8,128)}, u32[]{:S(2)}) copy-start(f32[2,448,256]{2,1,0:T(8,128)} %param.14) | copy-start | bytes 2752516
  (26 other events, 147.7 us)
